TPU v7x, 32 devices: a whole 2x2x4 slice. The times are simulated.
32 devices in a mesh: group: 2 (over y), seq: 4 (over z), tensor: 4 (over x, core).
Axes of the slice: x: 2, y: 2, z: 4, core: 2. Of those that a mesh axis runs over, the one named last changes fastest.
Arguments:
- query: bfloat16 [16, 7168], P(('group', 'seq'), 'tensor'), parts along dimension 0, may hold values from -5 to 5
- key_cache: bfloat16 [32, 256, 7168], P(('group', 'seq'), None, 'tensor'), parts along dimension 0, may hold values from -5 to 5
- value_cache: bfloat16 [32, 256, 7168], P(('group', 'seq'), None, 'tensor'), parts along dimension 0, may hold values from -6 to 6
- alibi_slopes: float32 [56], P('tensor'), may hold values from 0 to 1, as said below
- block_seq: int32 [32], P(('group', 'seq')), parts along dimension 0, may hold values from 0 to 7, as said below
- block_pos: int32 [32], P(('group', 'seq')), parts along dimension 0, may hold values from 0 to 2, as said below
- lengths: int32 [16], P('group'), parts along dimension 0, may hold values from 1 to 768, as said below
- out_weight: bfloat16 [7168, 14336], P('tensor', 'seq'), may hold values from -0.5 to 0.5
Outputs:
- mixed: bfloat16 [16, 14336], P(('group', 'tensor'), 'seq'), parts along dimension 0
There are 2 independent parts, one for each index of `group`. A program takes and returns all parts, laid end to end along the dimension named above; an argument that names none is the same for every part. Nothing has to cross between parts.
Inputs may be any that keep to these rules, and one draw needn't show every extreme that they name: `block_seq`: every sequence owns at least one block and at most 3; the blocks of sequence s have block_pos 0 to n_s - 1, each once. block_pos of a block is below the number of blocks its sequence owns. `lengths`: A sequence that owns n blocks has a length above 256 * (n - 1) and at most 256 * n. `alibi_slopes`: positive slopes.
All inputs are finite; a program needn't handle non-finite values.
Results may differ from a plain program's by a relative error of at most 0.0054.
Values may be sent and summed in bfloat16 or wider, within the bound.
No kernel may reach another device: no remote copies, remote signals or barrier semaphores. Data moves between devices by JAX's collectives and lax.ppermute only.
A program may use at most 64 MiB of HBM per device.

v0:
```python
import math
import jax
import jax.numpy as jnp
from jax import lax
from jax.sharding import PartitionSpec as P


def local(query, key_cache, value_cache, alibi_slopes, block_seq, block_pos, lengths, out_weight):
    heads = alibi_slopes.shape[0]
    features = query.shape[1]
    head_size = features // heads
    blocks_here = key_cache.shape[0]
    block_len = key_cache.shape[1]
    seq_count = lengths.shape[0]
    scale = 1.0 / math.sqrt(head_size)
    whole_query = lax.all_gather(query, "seq", axis=0, tiled=True)
    query_rows = jnp.take(whole_query, block_seq, axis=0).reshape(blocks_here, heads, head_size)
    keys = key_cache.reshape(blocks_here, block_len, heads, head_size)
    values = value_cache.reshape(blocks_here, block_len, heads, head_size)
    scores = (
        jnp.einsum("bthd,bhd->bht", keys, query_rows, preferred_element_type=jnp.float32) * scale
    )
    owner_length = lengths[block_seq]
    placed = block_pos[:, None] * block_len + jnp.arange(block_len, dtype=jnp.int32)[None, :]
    live = (placed < owner_length[:, None])[:, None, :]
    distance = (owner_length[:, None] - 1 - placed).astype(jnp.float32)
    scores = scores - alibi_slopes[None, :, None] * distance[:, None, :]
    scores = jnp.where(live, scores, -1e30)
    block_top = jnp.max(scores, axis=2)
    weights = jnp.where(live, jnp.exp(scores - block_top[:, :, None]), 0.0)
    block_total = jnp.sum(weights, axis=2)
    block_acc = jnp.einsum(
        "bht,bthd->bhd", weights.astype(jnp.bfloat16), values, preferred_element_type=jnp.float32
    )
    seq_ids = jnp.arange(seq_count, dtype=jnp.int32)
    owned = (block_seq[None, :] == seq_ids[:, None])[:, :, None]
    local_top = jnp.max(jnp.where(owned, block_top[None], -1e30), axis=1)
    factor = jnp.where(owned, jnp.exp(block_top[None] - local_top[:, None, :]), 0.0)
    local_total = jnp.sum(factor * block_total[None], axis=1)
    local_acc = jnp.einsum("sbh,bhd->shd", factor, block_acc, precision=lax.Precision.HIGHEST)
    tops, totals, accs = (
        lax.all_to_all(local_top[None], "seq", split_axis=1, concat_axis=0, tiled=True),
        lax.all_to_all(local_total[None], "seq", split_axis=1, concat_axis=0, tiled=True),
        lax.all_to_all(local_acc[None], "seq", split_axis=1, concat_axis=0, tiled=True),
    )
    best = jnp.max(tops, axis=0)
    scaling = jnp.exp(tops - best[None])
    home_total = jnp.sum(totals * scaling, axis=0)
    home_acc = jnp.sum(accs * scaling[..., None], axis=0)
    mine = (
        (home_acc / home_total[:, :, None])
        .astype(jnp.bfloat16)
        .reshape(home_acc.shape[0], features)
    )
    attention = lax.all_gather(mine, "seq", axis=0, tiled=True)
    mixed = lax.psum_scatter(
        jnp.dot(attention, out_weight, preferred_element_type=jnp.float32),
        "tensor",
        scatter_dimension=0,
        tiled=True,
    )
    return mixed.astype(jnp.bfloat16)


def solution(mesh):
    placed = (
        P(("group", "seq"), "tensor"),
        P(("group", "seq"), None, "tensor"),
        P(("group", "seq"), None, "tensor"),
        P("tensor"),
        P(("group", "seq")),
        P(("group", "seq")),
        P("group"),
        P("tensor", "seq"),
    )
    return jax.shard_map(
        local, mesh=mesh, in_specs=placed, out_specs=P(("group", "tensor"), "seq"), check_vma=False
    )
```

profile of v0, /device:TPU:0, one launch (start us, length us, event | category | flops | bytes accessed | tf_op | source)
XLA Modules:
  0.0 95.4 jit_solution(14486349411866468453)
XLA Ops:
  0.0 0.7 compare_select_fusion
  0.7 0.7 compare_and_fusion
  1.3 0.7 iota_compare_fusion
  2.1 0.6 gather_fusion
  2.7 0.7 broadcast_add_fusion
  3.5 15.1 %all-gather = bf16[4,2,1792]{2,1,0:T(2,128)(2,1)S(1)} all-gather(bf16[1,2,1792]{2,1,0:T(2,128)(2,1)} %bitcast.41), channel_id=1, replica_groups=mesh['group'=2,'seq'=4,'tensor'=4] {'seq'}, dimensions={0}, use_global_device_ids=true | all-gather | bytes 35840 | tf_op jit(solution)/shard_map/all_gather | solution.py:16
  18.6 0.6 gather_fusion.1
  19.2 6.0 %copy.49 = bf16[4,256,1792]{1,2,0:T(8,128)(2,1)} copy(bf16[4,256,1792]{2,1,0:T(8,128)(2,1)} %param.9) | data formatting | bytes 7340032 | tf_op args[1]
  25.3 2.6 %fusion.9 = f32[4,14,1,256]{3,2,1,0:T(1,128)S(1)} fusion(bf16[4,256,14,128]{1,3,2,0:T(8,128)(2,1)} %bitcast.33, bf16[4,14,128,1]{2,1,0,3:T(8,128)(2,1)S(1)} %select_bitcast_fusion), kind=kOutput, calls=%fused_computation.16 | convolution fusion | flops 3670016 | bytes 3741696 | tf_op jit(solution)/shard_map/bthd,bhd->bht/dot_general | solution.py:21
  28.1 0.7 copy.54
  28.8 4.7 %all-to-all-start.1 = ((f32[1,8,14]{2,0,1:T(1,128)}), f32[1,8,14]{2,0,1:T(1,128)S(1)}, u32[]{:S(2)}, u32[]{:S(2)}) async-start(f32[1,8,14]{2,0,1:T(1,128)} %copy.54), calls=%async_computation.1 | async-start | bytes 8192 | tf_op jit(solution)/shard_map/all_to_all | solution.py:42
  33.8 6.0 %copy.50 = bf16[4,256,1792]{1,2,0:T(8,128)(2,1)} copy(bf16[4,256,1792]{2,1,0:T(8,128)(2,1)} %param.10) | data formatting | bytes 7340032 | tf_op args[2]
  39.8 3.1 %fusion.2 = f32[4,14,1,128]{3,2,1,0:T(1,128)S(1)} fusion(bf16[4,256,14,128]{1,3,2,0:T(8,128)(2,1)} %bitcast.34, bf16[4,14,256,1]{2,0,1,3:T(4,128)(2,1)S(1)} %get-tuple-element.10), kind=kOutput, calls=%fused_computation.6 | convolution fusion | flops 3670016 | bytes 3727360 | tf_op jit(solution)/shard_map/bht,bthd->bhd/dot_general | solution.py:32
  43.3 0.7 copy.57
  44.0 5.1 %all-to-all-start.2 = ((f32[1,8,14]{2,0,1:T(1,128)}), f32[1,8,14]{2,0,1:T(1,128)S(1)}, u32[]{:S(2)}, u32[]{:S(2)}) async-start(f32[1,8,14]{2,0,1:T(1,128)} %copy.57), calls=%async_computation.2 | async-start | bytes 8192 | tf_op jit(solution)/shard_map/all_to_all | solution.py:43
  49.1 0.7 copy.51
  49.7 0.6 dynamic-slice
  51.0 3.7 %all-to-all-done.2 = f32[1,8,14]{2,0,1:T(1,128)S(1)} async-done(((f32[1,8,14]{2,0,1:T(1,128)}), f32[1,8,14]{2,0,1:T(1,128)S(1)}, u32[]{:S(2)}, u32[]{:S(2)}) %all-to-all-start.2) | async-done | bytes 480 | tf_op jit(solution)/shard_map/all_to_all | solution.py:43
  54.6 3.3 %all-to-all-start = ((f32[1,8,14,128]{3,0,2,1:T(1,128)}), f32[1,8,14,128]{3,0,2,1:T(1,128)S(1)}, u32[]{:S(2)}, u32[]{:S(2)}) async-start(f32[1,8,14,128]{3,0,2,1:T(1,128)} %copy.51), calls=%async_computation | async-start | bytes 114688 | tf_op jit(solution)/shard_map/all_to_all | solution.py:44
  58.2 5.5 %all-to-all-done = f32[1,8,14,128]{3,0,2,1:T(1,128)S(1)} async-done(((f32[1,8,14,128]{3,0,2,1:T(1,128)}), f32[1,8,14,128]{3,0,2,1:T(1,128)S(1)}, u32[]{:S(2)}, u32[]{:S(2)}) %all-to-all-start) | async-done | bytes 57376 | tf_op jit(solution)/shard_map/all_to_all | solution.py:44
  63.9 13.2 %all-gather.1 = bf16[4,2,1792]{2,1,0:T(2,128)(2,1)S(1)} all-gather(bf16[1,2,1792]{2,1,0:T(2,128)(2,1)S(1)} %fusion.15), channel_id=1, replica_groups=mesh['group'=2,'seq'=4,'tensor'=4] {'seq'}, dimensions={0}, use_global_device_ids=true | all-gather | bytes 35840 | tf_op jit(solution)/shard_map/all_gather | solution.py:55
  77.1 6.4 %fusion.20 = f32[8,3584]{1,0:T(8,128)S(1)} fusion(bf16[8,1792]{1,0:T(8,128)(2,1)S(1)} %reshape.152, bf16[1792,3584]{1,0:T(8,128)(2,1)} %param.15), kind=kOutput, calls=%fused_computation.41 | convolution fusion | flops 102760448 | bytes 12988416 | tf_op jit(solution)/shard_map/dot_general | solution.py:57
  83.5 11.3 %all-reduce = bf16[8,3584]{1,0:T(8,128)(2,1)S(1)} all-reduce(f32[8,3584]{1,0:T(8,128)S(1)} %fusion.20), channel_id=2, replica_groups=mesh['group'=2,'seq'=4,'tensor'=4] {'tensor'}, use_global_device_ids=true, to_apply=%region_7.8.clone | all-reduce | flops 28672 | bytes 172032
  94.7 0.6 dynamic-slice_convert_fusion
  (26 shorter events, 1.7 us)
Async XLA Ops:
  0.0 2.1 %copy-start = (s32[8]{0:T(128)S(1)}, s32[8]{0:T(128)}, u32[]{:S(2)}) copy-start(s32[8]{0:T(128)} %param.14) | copy-start | bytes 100
  25.2 2.7 %copy-start.1 = (f32[14]{0:T(128)S(1)}, f32[14]{0:T(128)}, u32[]{:S(2)}) copy-start(f32[14]{0:T(128)} %param.11) | copy-start | bytes 172
  28.8 15.2 %all-to-all-start.1 = ((f32[1,8,14]{2,0,1:T(1,128)}), f32[1,8,14]{2,0,1:T(1,128)S(1)}, u32[]{:S(2)}, u32[]{:S(2)}) async-start(f32[1,8,14]{2,0,1:T(1,128)} %copy.54), calls=%async_computation.1 | async-start | bytes 8192 | tf_op jit(solution)/shard_map/all_to_all | solution.py:42
  39.8 9.9 %copy-start.2 = (u32[32]{0:T(128)S(1)}, u32[32]{0:T(128)}, u32[]{:S(2)}) copy-start(u32[32]{0:T(128)} %constant.39) | copy-start | bytes 388
  44.0 10.7 %all-to-all-start.2 = ((f32[1,8,14]{2,0,1:T(1,128)}), f32[1,8,14]{2,0,1:T(1,128)S(1)}, u32[]{:S(2)}, u32[]{:S(2)}) async-start(f32[1,8,14]{2,0,1:T(1,128)} %copy.57), calls=%async_computation.2 | async-start | bytes 8192 | tf_op jit(solution)/shard_map/all_to_all | solution.py:43
  54.6 9.0 %all-to-all-start = ((f32[1,8,14,128]{3,0,2,1:T(1,128)}), f32[1,8,14,128]{3,0,2,1:T(1,128)S(1)}, u32[]{:S(2)}, u32[]{:S(2)}) async-start(f32[1,8,14,128]{3,0,2,1:T(1,128)} %copy.51), calls=%async_computation | async-start | bytes 114688 | tf_op jit(solution)/shard_map/all_to_all | solution.py:44
where the time goes:
time: 96.1 us; the launch traced here: 95.4 us
  blocking collectives  39.5 us (41%)
  local copies, waits for them, and re-layouts  16.7 us (17%)
  starting transfers between devices  13.1 us (14%)
  matrix products  12.5 us (13%)
  waiting for transfers between devices  9.12 us (9%)
  other arithmetic  3.75 us (4%)
    all_gather x1, blocking collectives, local(): whole_query = lax.all_gather(query, 'seq', axis=0, tiled=True)  15.1 us
    all_gather x1, blocking collectives, local(): attention = lax.all_gather(mine, 'seq', axis=0, tiled=True)  13.2 us
    unnamed x11, local copies, waits for them, and re-layouts  12.6 us
    unnamed x1, blocking collectives  11.3 us
    dot_general x1, matrix products, local(): jnp.dot(attention, out_weight, preferred_element_type=jnp.float32)  6.41 us
    all_to_all x1, waiting for transfers between devices, local(): lax.all_to_all(local_acc[None], 'seq', split_axis=1, concat_axis=0, tiled...  5.46 us
    all_to_all x1, starting transfers between devices, local(): lax.all_to_all(local_total[None], 'seq', split_axis=1, concat_axis=0, til...  5.09 us
    all_to_all x1, starting transfers between devices, local(): lax.all_to_all(local_top[None], 'seq', split_axis=1, concat_axis=0, tiled...  4.74 us
  transfers between devices with their start and end apart: 3, of which 2 were waited for; matrix products, arithmetic and copies ran while one was open for 13% of the time, Pallas kernels for 0%

commit v1 on v0

--- a/solution.py
+++ b/solution.py
@@ -13,7 +13,8 @@
     block_len = key_cache.shape[1]
     seq_count = lengths.shape[0]
     scale = 1.0 / math.sqrt(head_size)
-    whole_query = lax.all_gather(query, "seq", axis=0, tiled=True)
+    sent = jnp.stack([query] * lax.axis_size("seq"))
+    whole_query = jnp.concatenate(lax.all_to_all(sent, "seq", 0, 0), axis=0)
     query_rows = jnp.take(whole_query, block_seq, axis=0).reshape(blocks_here, heads, head_size)
     keys = key_cache.reshape(blocks_here, block_len, heads, head_size)
     values = value_cache.reshape(blocks_here, block_len, heads, head_size)

time: 96.1 us -> 90.1 us (0.938)
  blocking collectives: 39.5 us -> 24.4 us
  starting transfers between devices: 13.1 us -> 18.1 us
  waiting for transfers between devices: 9.12 us -> 11.7 us
  local copies, waits for them, and re-layouts: 16.7 us -> 18 us
    all_gather x1 -> x0, blocking collectives: 15.1 us -> none  [local(): whole_query = lax.all_gather(query, 'seq', axis=0, tiled=True)]
    all_to_all x0 -> x1, starting transfers between devices: none -> 6.35 us  [local(): whole_query = jnp.concatenate(lax.all_to_all(sent, 'seq', 0, 0), axis=0)]
    all_to_all x1, waiting for transfers between devices: 0.01 us -> 1.7 us  [local(): lax.all_to_all(local_top[None], 'seq', split_axis=1, concat_axis=0, tiled...]
    all_to_all x1, starting transfers between devices: 5.09 us -> 3.4 us  [local(): lax.all_to_all(local_total[None], 'seq', split_axis=1, concat_axis=0, til...]
    another operation x0 -> x1, local copies, waits for them, and re-layouts: none -> 1.32 us  [local(): sent = jnp.stack([query] * lax.axis_size('seq'))]
    unnamed x11 -> x10, local copies, waits for them, and re-layouts: 12.6 us -> 12.6 us
  transfers between devices with their start and end apart: 3 -> 4, of which waited for: 2 -> 3; matrix products, arithmetic and copies ran while one was open for 13% -> 24% of each run, Pallas kernels for 0% -> 0%
where the time goes in v1:
time: 90.1 us; the launch traced here: 89.2 us
  blocking collectives  24.4 us (27%)
  starting transfers between devices  18.1 us (20%)
  local copies, waits for them, and re-layouts  18 us (20%)
  matrix products  12.5 us (14%)
  waiting for transfers between devices  11.7 us (13%)
  other arithmetic  3.76 us (4%)
    all_gather x1, blocking collectives, local(): attention = lax.all_gather(mine, 'seq', axis=0, tiled=True)  13.2 us
    unnamed x10, local copies, waits for them, and re-layouts  12.6 us
    unnamed x1, blocking collectives  11.3 us
    dot_general x1, matrix products, local(): jnp.dot(attention, out_weight, preferred_element_type=jnp.float32)  6.41 us
    all_to_all x1, starting transfers between devices, local(): whole_query = jnp.concatenate(lax.all_to_all(sent, 'seq', 0, 0), axis=0)  6.35 us
    all_to_all x1, waiting for transfers between devices, local(): lax.all_to_all(local_acc[None], 'seq', split_axis=1, concat_axis=0, tiled...  5.46 us
    all_to_all x1, starting transfers between devices, local(): lax.all_to_all(local_top[None], 'seq', split_axis=1, concat_axis=0, tiled...  5.09 us
    all_to_all x1, waiting for transfers between devices, local(): lax.all_to_all(local_total[None], 'seq', split_axis=1, concat_axis=0, til...  4.5 us
  transfers between devices with their start and end apart: 4, of which 3 were waited for; matrix products, arithmetic and copies ran while one was open for 24% of the time, Pallas kernels for 0%

profile of v1, /device:TPU:0, one launch (start us, length us, event | category | flops | bytes accessed | tf_op | source)
XLA Modules:
  0.0 89.2 jit_solution(8895309502956765347)
XLA Ops:
  0.0 1.3 %stack.2 = bf16[4,2,1792]{2,1,0:T(2,128)(2,1)} broadcast(bf16[2,1792]{1,0:T(2,128)(2,1)} %param.8), dimensions={1,2} | broadcast | bytes 35840 | tf_op jit(solution)/shard_map/stack | solution.py:16
  1.3 6.3 %all-to-all-start = ((bf16[4,2,1792]{2,1,0:T(2,128)(2,1)}), bf16[4,2,1792]{2,1,0:T(2,128)(2,1)S(1)}, u32[]{:S(2)}, u32[]{:S(2)}) async-start(bf16[4,2,1792]{2,1,0:T(2,128)(2,1)} %stack.2), calls=%async_computation | async-start | bytes 57344 | tf_op jit(solution)/shard_map/all_to_all | solution.py:17
  7.7 0.7 compare_select_fusion
  8.3 0.7 compare_and_fusion
  9.0 0.6 gather_fusion
  9.7 0.7 broadcast_add_fusion
  10.5 0.7 iota_compare_fusion
  11.2 6.0 %copy.49 = bf16[4,256,1792]{1,2,0:T(8,128)(2,1)} copy(bf16[4,256,1792]{2,1,0:T(8,128)(2,1)} %param.9) | data formatting | bytes 7340032 | tf_op args[1]
  17.2 6.0 %copy.50 = bf16[4,256,1792]{1,2,0:T(8,128)(2,1)} copy(bf16[4,256,1792]{2,1,0:T(8,128)(2,1)} %param.10) | data formatting | bytes 7340032 | tf_op args[2]
  25.1 2.6 %fusion.9 = f32[4,14,1,256]{3,2,1,0:T(1,128)S(1)} fusion(bf16[4,256,14,128]{1,3,2,0:T(8,128)(2,1)} %bitcast.33, bf16[4,14,128,1]{2,1,0,3:T(8,128)(2,1)S(1)} %select_bitcast_fusion), kind=kOutput, calls=%fused_computation.16 | convolution fusion | flops 3670016 | bytes 3741696 | tf_op jit(solution)/shard_map/bthd,bhd->bht/dot_general | solution.py:22
  28.2 0.7 copy.54
  28.8 5.1 %all-to-all-start.2 = ((f32[1,8,14]{2,0,1:T(1,128)}), f32[1,8,14]{2,0,1:T(1,128)S(1)}, u32[]{:S(2)}, u32[]{:S(2)}) async-start(f32[1,8,14]{2,0,1:T(1,128)} %copy.54), calls=%async_computation.2 | async-start | bytes 8192 | tf_op jit(solution)/shard_map/all_to_all | solution.py:43
  33.9 3.1 %fusion.2 = f32[4,14,1,128]{3,2,1,0:T(1,128)S(1)} fusion(bf16[4,256,14,128]{1,3,2,0:T(8,128)(2,1)} %bitcast.32, bf16[4,14,256,1]{2,0,1,3:T(4,128)(2,1)S(1)} %get-tuple-element.10), kind=kOutput, calls=%fused_computation.6 | convolution fusion | flops 3670016 | bytes 3727360 | tf_op jit(solution)/shard_map/bht,bthd->bhd/dot_general | solution.py:33
  37.1 0.7 copy.57
  37.8 1.7 %all-to-all-done.2 = f32[1,8,14]{2,0,1:T(1,128)S(1)} async-done(((f32[1,8,14]{2,0,1:T(1,128)}), f32[1,8,14]{2,0,1:T(1,128)S(1)}, u32[]{:S(2)}, u32[]{:S(2)}) %all-to-all-start.2) | async-done | bytes 480 | tf_op jit(solution)/shard_map/all_to_all | solution.py:43
  39.5 3.4 %all-to-all-start.3 = ((f32[1,8,14]{2,0,1:T(1,128)}), f32[1,8,14]{2,0,1:T(1,128)S(1)}, u32[]{:S(2)}, u32[]{:S(2)}) async-start(f32[1,8,14]{2,0,1:T(1,128)} %copy.57), calls=%async_computation.3 | async-start | bytes 8192 | tf_op jit(solution)/shard_map/all_to_all | solution.py:44
  43.3 0.7 copy.51
  44.0 4.5 %all-to-all-done.3 = f32[1,8,14]{2,0,1:T(1,128)S(1)} async-done(((f32[1,8,14]{2,0,1:T(1,128)}), f32[1,8,14]{2,0,1:T(1,128)S(1)}, u32[]{:S(2)}, u32[]{:S(2)}) %all-to-all-start.3) | async-done | bytes 480 | tf_op jit(solution)/shard_map/all_to_all | solution.py:44
  48.5 3.3 %all-to-all-start.1 = ((f32[1,8,14,128]{3,0,2,1:T(1,128)}), f32[1,8,14,128]{3,0,2,1:T(1,128)S(1)}, u32[]{:S(2)}, u32[]{:S(2)}) async-start(f32[1,8,14,128]{3,0,2,1:T(1,128)} %copy.51), calls=%async_computation.1 | async-start | bytes 114688 | tf_op jit(solution)/shard_map/all_to_all | solution.py:45
  52.0 5.5 %all-to-all-done.1 = f32[1,8,14,128]{3,0,2,1:T(1,128)S(1)} async-done(((f32[1,8,14,128]{3,0,2,1:T(1,128)}), f32[1,8,14,128]{3,0,2,1:T(1,128)S(1)}, u32[]{:S(2)}, u32[]{:S(2)}) %all-to-all-start.1) | async-done | bytes 57376 | tf_op jit(solution)/shard_map/all_to_all | solution.py:45
  57.7 13.2 %all-gather = bf16[4,2,1792]{2,1,0:T(2,128)(2,1)S(1)} all-gather(bf16[1,2,1792]{2,1,0:T(2,128)(2,1)S(1)} %fusion.15), channel_id=1, replica_groups=mesh['group'=2,'seq'=4,'tensor'=4] {'seq'}, dimensions={0}, use_global_device_ids=true | all-gather | bytes 35840 | tf_op jit(solution)/shard_map/all_gather | solution.py:56
  70.9 6.4 %fusion.20 = f32[8,3584]{1,0:T(8,128)S(1)} fusion(bf16[8,1792]{1,0:T(8,128)(2,1)S(1)} %reshape.156, bf16[1792,3584]{1,0:T(8,128)(2,1)} %param.15), kind=kOutput, calls=%fused_computation.41 | convolution fusion | flops 102760448 | bytes 12988416 | tf_op jit(solution)/shard_map/dot_general | solution.py:58
  77.3 11.3 %all-reduce = bf16[8,3584]{1,0:T(8,128)(2,1)S(1)} all-reduce(f32[8,3584]{1,0:T(8,128)S(1)} %fusion.20), channel_id=2, replica_groups=mesh['group'=2,'seq'=4,'tensor'=4] {'tensor'}, use_global_device_ids=true, to_apply=%region_7.8.clone | all-reduce | flops 28672 | bytes 172032
  88.6 0.6 dynamic-slice_convert_fusion
  (28 shorter events, 2.9 us)
Async XLA Ops:
  0.0 9.0 %copy-start = (s32[8]{0:T(128)S(1)}, s32[8]{0:T(128)}, u32[]{:S(2)}) copy-start(s32[8]{0:T(128)} %param.14) | copy-start | bytes 100
  1.3 23.1 %all-to-all-start = ((bf16[4,2,1792]{2,1,0:T(2,128)(2,1)}), bf16[4,2,1792]{2,1,0:T(2,128)(2,1)S(1)}, u32[]{:S(2)}, u32[]{:S(2)}) async-start(bf16[4,2,1792]{2,1,0:T(2,128)(2,1)} %stack.2), calls=%async_computation | async-start | bytes 57344 | tf_op jit(solution)/shard_map/all_to_all | solution.py:17
  17.2 6.0 %copy-start.2 = (u32[32]{0:T(128)S(1)}, u32[32]{0:T(128)}, u32[]{:S(2)}) copy-start(u32[32]{0:T(128)} %constant.39) | copy-start | bytes 388
  23.2 4.6 %copy-start.1 = (f32[14]{0:T(128)S(1)}, f32[14]{0:T(128)}, u32[]{:S(2)}) copy-start(f32[14]{0:T(128)} %param.11) | copy-start | bytes 172
  28.8 10.7 %all-to-all-start.2 = ((f32[1,8,14]{2,0,1:T(1,128)}), f32[1,8,14]{2,0,1:T(1,128)S(1)}, u32[]{:S(2)}, u32[]{:S(2)}) async-start(f32[1,8,14]{2,0,1:T(1,128)} %copy.54), calls=%async_computation.2 | async-start | bytes 8192 | tf_op jit(solution)/shard_map/all_to_all | solution.py:43
  39.5 9.0 %all-to-all-start.3 = ((f32[1,8,14]{2,0,1:T(1,128)}), f32[1,8,14]{2,0,1:T(1,128)S(1)}, u32[]{:S(2)}, u32[]{:S(2)}) async-start(f32[1,8,14]{2,0,1:T(1,128)} %copy.57), calls=%async_computation.3 | async-start | bytes 8192 | tf_op jit(solution)/shard_map/all_to_all | solution.py:44
  48.5 9.0 %all-to-all-start.1 = ((f32[1,8,14,128]{3,0,2,1:T(1,128)}), f32[1,8,14,128]{3,0,2,1:T(1,128)S(1)}, u32[]{:S(2)}, u32[]{:S(2)}) async-start(f32[1,8,14,128]{3,0,2,1:T(1,128)} %copy.51), calls=%async_computation.1 | async-start | bytes 114688 | tf_op jit(solution)/shard_map/all_to_all | solution.py:45
